TPU v7x, 32 devices: a whole 2x2x4 slice. The times are simulated.
32 devices in a mesh: dp: 16 (over z, y, x), mp: 2 (over core).
Axes of the slice: x: 2, y: 2, z: 4, core: 2. Of those that a mesh axis runs over, the one named last changes fastest.
Arguments:
- normed: bfloat16 [6144, 2048], P(('dp', 'mp')), may hold values from -12 to 12
- key_grad: bfloat16 [6144, 512], P('dp', 'mp'), may hold values from -0.078125 to 0.078125
- stale: bfloat16 [16, 2048, 512], P('dp', None, 'mp'), may hold values from -1.5 to 1.5
- worker_flag: int32 [16], P('dp'), may hold values 0 or 1
- block_mask: int32 [16, 4], P('dp'), may hold values 0 or 1
- aggregate: float32 [2048, 512], P('dp', 'mp'), may hold values from -6 to 6
- master: float32 [2048, 512], P('dp', 'mp'), may hold values from -0.125 to 0.125
- moment_one: float32 [2048, 512], P('dp', 'mp'), may hold values from -6 to 6
- moment_two: float32 [2048, 512], P('dp', 'mp'), may hold values from 0.5 to 4
Outputs:
- new_aggregate: float32 [2048, 512], P('dp', 'mp')
- new_master: float32 [2048, 512], P('dp', 'mp')
- new_moment_one: float32 [2048, 512], P('dp', 'mp')
- new_moment_two: float32 [2048, 512], P('dp', 'mp')
- weights: bfloat16 [2048, 512], P(None, 'mp')
- new_stale: bfloat16 [16, 2048, 512], P('dp', None, 'mp')
All inputs are finite; a program needn't handle non-finite values. No bound on the sum of `worker_flag` on one device may be relied on, other than what follows from the above.
Results may differ from a plain program's by a relative error of at most 0.0004.
Values may be sent and summed in bfloat16 or wider, within the bound.
A program may use at most 64 MiB of HBM per device.

v0:
```python
import functools
import math

import jax
import jax.numpy as jnp
from jax import lax
from jax.experimental import pallas as pl
from jax.experimental.pallas import tpu as pltpu
from jax.sharding import PartitionSpec as P

H = 512
BLOCKS = 4
STEP = 10


beta_one = 0.9
beta_two = 0.95
learn_rate = 0.001
decay_rate = 0.1
epsilon = 1e-08

LANES = 128
WIRE = jnp.int16
FINEST = 2.0**14
LEVELS = 1092.0
MESH = pl.DeviceIdType.MESH


def grid_of(workers):
    inner = max(i for i in range(1, math.isqrt(workers // 2) + 1) if workers % (i * i) == 0)
    return workers // (inner * inner), inner


def encode(values):
    size = jnp.log2(1.0 + jnp.abs(values) * FINEST)
    code = jnp.minimum(size * LEVELS + 0.5, 32767.0).astype(jnp.int32)
    return jnp.where(values < 0, -code, code).astype(jnp.int16)


def decode(codes):
    code = codes.astype(jnp.int32).astype(jnp.float32)
    size = (jnp.exp2(jnp.abs(code) * (1.0 / LEVELS)) - 1.0) * (1.0 / FINEST)
    return jnp.where(code < 0, -size, size)


def kernel(
    zs, ins, mps, width,
    normed, key_grad, stale, flag, far_mask, aggregate, master, moment_one, moment_two,
    out_aggregate, out_master, out_one, out_two, out_weights, kept,
    mine, theirs, kgrad, old, states,
    part, wire, got_one, sum_one, wire_two, got_two, wire_three, own_sum, got_three,
    mask, load_sem, mp_send, mp_recv, one_send, one_recv, two_send, two_recv,
    three_send, three_recv, gz_send, gz_recv, gs_send, gs_recv, gl_send, gl_recv,
    gd_send, gd_recv,
):
    me = lax.axis_index("dp")
    core = lax.axis_index("mp")
    z, a, b = me // (ins * ins), lax.rem(me // ins, ins), lax.rem(me, ins)
    tokens = normed.shape[0]
    slab = normed.shape[1] // zs
    rows = slab // (ins * ins)
    cols = key_grad.shape[1]

    def at(zz, aa, bb):
        return {"dp": (zz * ins + aa) * ins + bb}

    def hop(base, j, size):
        return lax.rem(base + j, size)

    loads = [
        pltpu.make_async_copy(src, dst, load_sem.at[i])
        for i, (src, dst) in enumerate(
            [(far_mask, mask), (normed, mine), (key_grad, kgrad), (stale.at[0], old)]
            + [(src, states.at[i]) for i, src in enumerate((aggregate, master, moment_one, moment_two))]
        )
    ]
    for load in loads:
        load.start()

    peers = [{"mp": hop(core, j, mps)} for j in range(1, mps)]
    peers += [at(hop(z, j, zs), a, b) for j in range(1, zs)]
    peers += [at(z, hop(a, j, ins), b) for j in range(1, ins)]
    peers += [at(z, a, hop(b, j, ins)) for j in range(1, ins)]
    barrier = pltpu.get_barrier_semaphore()
    for peer in peers:
        pl.semaphore_signal(barrier, inc=1, device_id=peer, device_id_type=MESH)
    pl.semaphore_wait(barrier, len(peers))

    pending = []

    def send(src, dst, send_sem, recv_sem, peer):
        copy = pltpu.make_async_remote_copy(
            src_ref=src, dst_ref=dst, send_sem=send_sem, recv_sem=recv_sem,
            device_id=peer, device_id_type=MESH,
        )
        copy.start()
        pending.append(copy)
        return copy

    order = list(range(1, zs)) + [0]
    shared = {}
    for k in order:
        columns = pl.ds(pl.multiple_of(hop(z, k, zs) * slab, slab), slab)
        shared[k] = [
            send(
                normed.at[:, columns], theirs.at[j - 1, :, columns],
                mp_send.at[k, j - 1], mp_recv.at[k, j - 1], {"mp": hop(core, j, mps)},
            )
            for j in range(1, mps)
        ]

    loads[0].wait()
    block = (core * cols + lax.broadcasted_iota(jnp.int32, (1, cols), 1)) // width
    trig = jnp.zeros((1, cols), jnp.int32)
    for i in range(BLOCKS):
        trig = trig + jnp.where(block == i, flag[0] * mask[0, i], 0)
    weight = trig.astype(jnp.float32)

    for load in loads[1:4]:
        load.wait()

    def compute(k):
        base = pl.multiple_of(hop(z, k, zs) * slab, slab)
        columns = pl.ds(base, slab)

        def product(left, owner):
            held = kgrad[pl.ds(pl.multiple_of(owner * tokens, tokens), tokens), :]
            return lax.dot_general(
                left, held, (((0,), (0,)), ((), ())), preferred_element_type=jnp.float32
            )

        grad = product(mine[:, columns], core)
        for j in range(1, mps):
            shared[k][j - 1].wait_recv()
            grad = grad + product(theirs[j - 1, :, columns], hop(core, mps - j, mps))
        before = old[pl.ds(base, slab), :].astype(jnp.float32)
        kept[pl.ds(base, slab), :] = jnp.where(trig > 0, grad, before).astype(jnp.bfloat16)
        change = weight * (grad - before)
        for s in range(2):
            piece = change[:, s * LANES:(s + 1) * LANES].reshape(ins, ins, rows, LANES)
            part[s, k] = piece

    firsts, seconds, thirds = {}, {}, {}
    source = part if WIRE == jnp.float32 else wire
    source_two = sum_one if WIRE == jnp.float32 else wire_two

    def send_one(k):
        firsts[k] = []
        for j in range(1, ins):
            bb, aa = hop(b, j, ins), hop(a, j, ins)
            if WIRE != jnp.float32:
                wire[0, k, :, bb] = encode(part[0, k, :, bb])
                wire[1, k, aa] = encode(part[1, k, aa])
            firsts[k].append((
                send(source.at[0, k, :, bb], got_one.at[0, k, j - 1],
                     one_send.at[0, k, j - 1], one_recv.at[0, k, j - 1], at(z, a, bb)),
                send(source.at[1, k, aa], got_one.at[1, k, j - 1],
                     one_send.at[1, k, j - 1], one_recv.at[1, k, j - 1], at(z, aa, b)),
            ))

    def send_two(k):
        for s in range(2):
            total = part[0, k, :, b] if s == 0 else part[1, k, a]
            for j in range(1, ins):
                firsts[k][j - 1][s].wait_recv()
                total = total + decode(got_one[s, k, j - 1])
            sum_one[s, k] = total
        seconds[k] = []
        for j in range(1, ins):
            bb, aa = hop(b, j, ins), hop(a, j, ins)
            if WIRE != jnp.float32:
                wire_two[0, k, aa] = encode(sum_one[0, k, aa])
                wire_two[1, k, bb] = encode(sum_one[1, k, bb])
            seconds[k].append((
                send(source_two.at[0, k, aa], got_two.at[0, k, j - 1],
                     two_send.at[0, k, j - 1], two_recv.at[0, k, j - 1], at(z, aa, b)),
                send(source_two.at[1, k, bb], got_two.at[1, k, j - 1],
                     two_send.at[1, k, j - 1], two_recv.at[1, k, j - 1], at(z, a, bb)),
            ))

    def send_three(k):
        for s in range(2):
            total = sum_one[s, k, a if s == 0 else b]
            for j in range(1, ins):
                seconds[k][j - 1][s].wait_recv()
                total = total + decode(got_two[s, k, j - 1])
            if k == 0:
                own_sum[s] = total
            else:
                wire_three[k - 1, s] = encode(total)
        if k:
            thirds[k] = send(wire_three.at[k - 1], got_three.at[k - 1],
                             three_send.at[k - 1], three_recv.at[k - 1], at(hop(z, k, zs), a, b))

    compute(order[0])
    send_one(order[0])
    for i in range(1, zs + 2):
        if i < zs:
            compute(order[i])
            send_one(order[i])
        if 0 <= i - 1 < zs:
            send_two(order[i - 1])
        if 0 <= i - 2 < zs:
            send_three(order[i - 2])

    for load in loads[4:]:
        load.wait()
    for k in range(1, zs):
        thirds[k].wait_recv()
    for s in range(2):
        here = pl.ds(s * LANES, LANES)
        total = own_sum[s]
        for k in range(1, zs):
            total = total + decode(got_three[k - 1, s])
        new_aggregate = states[0, :, here] + total
        out_aggregate[:, here] = new_aggregate
        new_one = beta_one * states[2, :, here] + (1.0 - beta_one) * new_aggregate
        new_two = beta_two * states[3, :, here] + (1.0 - beta_two) * new_aggregate * new_aggregate
        out_one[:, here] = new_one
        out_two[:, here] = new_two
        first_hat = new_one / (1.0 - beta_one**STEP)
        second_hat = new_two / (1.0 - beta_two**STEP)
        update = first_hat / (jnp.sqrt(second_hat) + epsilon)
        held = states[1, :, here]
        new_master = held - learn_rate * (update + decay_rate * held)
        out_master[:, here] = new_master
        out_weights[z, a, b, :, here] = new_master.astype(jnp.bfloat16)

    halves = [pl.ds(s * LANES, LANES) for s in range(2)]
    spread = {
        k: send(out_weights.at[z, a, b], out_weights.at[z, a, b],
                gz_send.at[k - 1], gz_recv.at[k - 1], at(hop(z, k, zs), a, b))
        for k in range(1, zs)
    }
    shorts, longs, directs = {}, {}, {}

    def gather_all(k, zz):
        ref = out_weights.at[zz, a, b]
        directs[k] = [
            send(ref, ref, gd_send.at[k, j - 1], gd_recv.at[k, j - 1],
                 at(z, hop(a, j // ins, ins), hop(b, j % ins, ins)))
            for j in range(1, ins * ins)
        ]

    def gather_short(k):
        zz = hop(z, zs - k, zs)
        if k:
            spread[k].wait_recv()
        shorts[k] = []
        if k >= zs - 2:
            return gather_all(k, zz)
        for j in range(1, ins):
            bb, aa = hop(b, j, ins), hop(a, j, ins)
            for s, peer in ((0, at(z, aa, b)), (1, at(z, a, bb))):
                ref = out_weights.at[zz, a, b, :, halves[s]]
                shorts[k].append(
                    send(ref, ref, gs_send.at[s, k, j - 1], gs_recv.at[s, k, j - 1], peer)
                )

    def gather_long(k):
        zz = hop(z, zs - k, zs)
        for copy in shorts[k]:
            copy.wait_recv()
        longs[k] = []
        if k >= zs - 2:
            return
        for j in range(1, ins):
            bb, aa = hop(b, j, ins), hop(a, j, ins)
            for s, peer in ((0, at(z, a, bb)), (1, at(z, aa, b))):
                ref = (out_weights.at[zz, :, b, :, halves[0]] if s == 0
                       else out_weights.at[zz, a, :, :, halves[1]])
                longs[k].append(
                    send(ref, ref, gl_send.at[s, k, j - 1], gl_recv.at[s, k, j - 1], peer)
                )

    turn = list(range(zs))
    for i in range(zs + 1):
        if i < zs:
            gather_short(turn[i])
        if i >= 1:
            gather_long(turn[i - 1])
    for k in turn:
        for copy in longs[k] + directs.get(k, []):
            copy.wait_recv()
    for copy in pending:
        copy.wait_send()


def write_out(*refs):
    copies = [
        pltpu.make_async_copy(src, dst, refs[12].at[i])
        for i, (src, dst) in enumerate(zip(refs[:6], refs[6:12]))
    ]
    for copy in reversed(copies):
        copy.start()
    for copy in copies:
        copy.wait()


def on_device(
    workers, mps,
    normed, key_grad, stale, worker_flag, block_mask, aggregate, master, moment_one, moment_two
):
    zs, ins = grid_of(workers)
    tokens, depth = normed.shape
    cols = key_grad.shape[1]
    rows = aggregate.shape[0]
    f32, bf16 = jnp.float32, jnp.bfloat16
    dma = pltpu.SemaphoreType.DMA
    hbm = pl.BlockSpec(memory_space=pltpu.HBM)
    vmem = pl.BlockSpec(memory_space=pltpu.VMEM)
    far = functools.partial(pltpu.with_memory_space_constraint, memory_space=pltpu.HBM)
    smem = pl.BlockSpec(memory_space=pltpu.SMEM)
    state = jax.ShapeDtypeStruct((rows, cols), f32)
    one = (2, zs, ins, ins, rows, LANES)
    two = (2, zs, ins, rows, LANES)
    coded = WIRE != f32
    tiny = (1, 1, 1, 1, 8, LANES)
    results = pl.pallas_call(
        functools.partial(kernel, zs, ins, mps, H // BLOCKS),
        out_shape=(
            state, state, state, state,
            jax.ShapeDtypeStruct((zs, ins, ins, rows, cols), bf16),
            jax.ShapeDtypeStruct((depth, cols), bf16),
        ),
        in_specs=[hbm] * 3 + [smem] + [hbm] * 5,
        out_specs=(vmem,) * 6,
        scratch_shapes=[
            pltpu.VMEM((tokens, depth), bf16),
            pltpu.VMEM((mps - 1, tokens, depth), bf16),
            pltpu.VMEM(key_grad.shape, bf16),
            pltpu.VMEM((depth, cols), bf16),
            pltpu.VMEM((4, rows, cols), f32),
            pltpu.VMEM(one, f32),
            pltpu.VMEM(one if coded else tiny, WIRE),
            pltpu.VMEM((2, zs, ins - 1, ins, rows, LANES), WIRE),
            pltpu.VMEM(two, f32),
            pltpu.VMEM(two if coded else tiny[1:], WIRE),
            pltpu.VMEM((2, zs, ins - 1, rows, LANES), WIRE),
            pltpu.VMEM((zs - 1, 2, rows, LANES), WIRE),
            pltpu.VMEM((2, rows, LANES), f32),
            pltpu.VMEM((zs - 1, 2, rows, LANES), WIRE),
            pltpu.SMEM(block_mask.shape, jnp.int32),
            dma((8,)),
            dma((zs, mps - 1)), dma((zs, mps - 1)),
            dma((2, zs, ins - 1)), dma((2, zs, ins - 1)),
            dma((2, zs, ins - 1)), dma((2, zs, ins - 1)),
            dma((zs - 1,)), dma((zs - 1,)),
            dma((zs - 1,)), dma((zs - 1,)),
            dma((2, zs, ins - 1)), dma((2, zs, ins - 1)),
            dma((2, zs, ins - 1)), dma((2, zs, ins - 1)),
            dma((zs, ins * ins - 1)), dma((zs, ins * ins - 1)),
        ],
        compiler_params=pltpu.CompilerParams(
            collective_id=0, has_side_effects=True, vmem_limit_bytes=48 * 1024 * 1024
        ),
    )(
        far(normed), far(key_grad), far(stale), worker_flag, far(block_mask),
        far(aggregate), far(master), far(moment_one), far(moment_two),
    )
    results = results[:4] + (results[4].reshape(depth, cols), results[5])
    results = pl.pallas_call(
        write_out,
        out_shape=tuple(pltpu.HBM(x.shape, x.dtype) for x in results),
        in_specs=[vmem] * 6,
        out_specs=(hbm,) * 6,
        scratch_shapes=[dma((6,))],
        compiler_params=pltpu.CompilerParams(vmem_limit_bytes=2 * 1024 * 1024),
    )(*results)
    return results[:5] + (results[5][None],)


def solution(mesh):
    placed = (
        P(("dp", "mp"), None),
        P("dp", "mp"),
        P("dp", None, "mp"),
        P("dp"),
        P("dp", None),
        P("dp", "mp"),
        P("dp", "mp"),
        P("dp", "mp"),
        P("dp", "mp"),
    )
    return jax.shard_map(
        functools.partial(on_device, mesh.shape["dp"], mesh.shape["mp"]),
        mesh=mesh,
        in_specs=placed,
        out_specs=(
            P("dp", "mp"),
            P("dp", "mp"),
            P("dp", "mp"),
            P("dp", "mp"),
            P(None, "mp"),
            P("dp", None, "mp"),
        ),
        check_vma=False,
    )
```

profile of v0, /device:TPU:0, one launch (start us, length us, event | category | flops | bytes accessed | tf_op | source)
XLA Modules:
  0.0 41.0 jit_solution(15964786131644013481)
XLA Ops:
  1.3 38.2 %shard_map.136 = (f32[128,256]{1,0:T(8,128)S(1)}, f32[128,256]{1,0:T(8,128)S(1)}, f32[128,256]{1,0:T(8,128)S(1)}, f32[128,256]{1,0:T(8,128)S(1)}, bf16[4,2,2,128...) custom-call(bf16[192,2048]{1,0:T(8,128)(2,1)} %normed.1, bf16[384,256]{1,0:T(8,128)(2,1)} %key_grad.1, ...), custom_call_target="tpu_custom_call" | custom-call | tf_op jit(solution)/shard_map/pallas_call | solution.py:319
  39.5 1.5 %shard_map.137 = (f32[128,256]{1,0:T(8,128)}, f32[128,256]{1,0:T(8,128)}, f32[128,256]{1,0:T(8,128)}, f32[128,256]{1,0:T(8,128)}, bf16[2048,256]{1,0:T(8,128)(2,1)}, /*index=5*/bf16[2048,256]{1,0:T(8,128)(2,1)}) custom-call(f32[128,256]{1,0:T(8,128)S(1)} %get-tuple-element.18.refs_0_, f32[128,256]{1,0:T(8,128)S(1)} %get-tuple-element.19.refs_1_, ...), custom_call_target="tpu_custom_call" | custom-call | tf_op jit(solution)/shard_map/pallas_call | solution.py:362
where the time goes:
time: 41.2 us; the launch traced here: 41 us
  Pallas kernels  39.7 us (96%)
  between operations  1.29 us (3%)
    pallas_call x1, Pallas kernels, on_device(): pl.pallas_call(functools.partial(kernel, zs, ins, mps, H // BLOCKS), out_...  38.2 us
    pallas_call x1, Pallas kernels, on_device(): pl.pallas_call(write_out, out_shape=tuple((pltpu.HBM(x.shape, x.dtype) fo...  1.54 us

commit v1 on v0

v1 whole, which is shorter than its diff:
```python
import contextlib
import functools
import math

import jax
import jax.numpy as jnp
from jax import lax
from jax.experimental import pallas as pl
from jax.experimental.pallas import tpu as pltpu
from jax.sharding import PartitionSpec as P

H = 512
BLOCKS = 4
STEP = 10


beta_one = 0.9
beta_two = 0.95
learn_rate = 0.001
decay_rate = 0.1
epsilon = 1e-08

LANES = 128
WIRE = jnp.int16
FINEST = 2.0**14
LEVELS = 1092.0
MESH = pl.DeviceIdType.MESH


def grid_of(workers):
    inner = max(i for i in range(1, math.isqrt(workers // 2) + 1) if workers % (i * i) == 0)
    return workers // (inner * inner), inner


def encode(values):
    size = jnp.log2(1.0 + jnp.abs(values) * FINEST)
    code = jnp.minimum(size * LEVELS + 0.5, 32767.0).astype(jnp.int32)
    return jnp.where(values < 0, -code, code).astype(jnp.int16)


def decode(codes):
    code = codes.astype(jnp.int32).astype(jnp.float32)
    size = (jnp.exp2(jnp.abs(code) * (1.0 / LEVELS)) - 1.0) * (1.0 / FINEST)
    return jnp.where(code < 0, -size, size)


OWN = 4
SPLIT = 1
EARLY = 8
ZORDER = (1, 2, 3)


def scope(name):
    return contextlib.nullcontext()


STEPS = (
    "W0", "C0", "x0", "C1", "R0", "d0", "X1", "C2", "X2", "C3", "X3", "V0",
    "Z0", "Z1", "Z2", "Y0", "Y1", "B0", "X4", "Y2", "Y3", "Y4",
)
GATHER = (
    "B0", "A0", "D0", "F0", "D1", "D3", "D2",
)
GATHER_OTHER = (
    "B0", "A0", "D0", "F0", "D1", "D3", "D2",
)


def early_rows(rows, ins):
    size = rows // EARLY if EARLY else 0
    return 0 if size % 16 or (ins * ins - 1) * size > rows else size


def flip(base, j, size):
    if size & (size - 1):
        return lax.rem(base + j, size)
    bit = 1
    while bit < size:
        if j & bit:
            base = base + bit - 2 * bit * lax.rem(base // bit, 2)
        bit *= 2
    return base


def kernel(
    zs, ins, mps, width,
    normed, key_grad, stale, flag, far_mask, aggregate, master, moment_one, moment_two,
    out_aggregate, out_master, out_one, out_two, full, kept,
    mine, theirs, kgrad, old, states, acc,
    part, wire, got_one, sum_one, wire_two, got_two, wire_three, own_sum, got_three,
    early, got_early, part_b, wire_b, one_b, sum_b, two_b, got_b, got_all, got_all_b,
    mask, up, down, turn, load_sem, mp_send, mp_recv, one_send, one_recv, two_send, two_recv,
    three_send, three_recv, gz_send, gz_recv, gs_send, gs_recv, gl_send, gl_recv,
    gd_send, gd_recv, early_send, early_recv, ge_send, ge_recv, gf_send, gf_recv,
):
    me = lax.axis_index("dp")
    core = lax.axis_index("mp")
    z, a, b = me // (ins * ins), lax.rem(me // ins, ins), lax.rem(me, ins)
    tokens = normed.shape[0]
    slab = normed.shape[1] // zs
    rows = slab // (ins * ins)
    cut = early_rows(rows, ins)
    late = pl.ds(cut, rows - cut)
    cols = key_grad.shape[1]

    def at(zz, aa, bb):
        return {"dp": (zz * ins + aa) * ins + bb}

    def hop(base, j, size):
        return lax.rem(base + j, size)

    loads = [
        pltpu.make_async_copy(src, dst, load_sem.at[i])
        for i, (src, dst) in enumerate(
            [(normed, mine), (key_grad, kgrad), (far_mask, mask), (stale.at[0], old)]
        )
    ]
    for load in loads:
        load.start()
    for i, src in enumerate((aggregate, master, moment_one, moment_two)):
        pltpu.make_async_copy(src, states.at[i], load_sem.at[4]).start()

    peers = [{"mp": hop(core, j, mps)} for j in range(1, mps)]
    peers += [at(z, hop(a, j, ins), b) for j in range(1, ins)]
    peers += [at(z, a, hop(b, j, ins)) for j in range(1, ins)]
    barrier = pltpu.get_barrier_semaphore()

    def signal(sem, peer):
        pl.semaphore_signal(sem, inc=1, device_id=peer, device_id_type=MESH)

    def inform(low, high, sem, step, wait):
        @pl.when((z >= low) & (z <= high))
        def _():
            if wait:
                pl.semaphore_wait(sem, 1)
            if step:
                signal(sem, at(z + step, a, b))

    for peer in peers:
        signal(barrier, peer)
    inform(1, zs - 1, barrier, -1, False)
    inform(0, zs - 2, barrier, 1, False)

    def arrive(sem, ref):
        pltpu.make_async_copy(ref, ref, sem).wait()

    def send(src, dst, send_sem, recv_sem, peer):
        copy = pltpu.make_async_remote_copy(
            src_ref=src, dst_ref=dst, send_sem=send_sem, recv_sem=recv_sem,
            device_id=peer, device_id_type=MESH,
        )
        copy.start()
        return copy

    order = list(range(zs - 1, -1, -1))

    def product(left, owner):
        held = kgrad[pl.ds(pl.multiple_of(owner * tokens, tokens), tokens), :]
        return lax.dot_general(
            left, held, (((0,), (0,)), ((), ())), preferred_element_type=jnp.float32
        )

    def columns_of(k):
        return pl.ds(pl.multiple_of(flip(z, k, zs) * slab, slab), slab)

    with scope("loads"):
        loads[0].wait()
    with scope("barrier"):
        pl.semaphore_wait(barrier, len(peers) + jnp.where(z > 0, 1, 0) + jnp.where(z < zs - 1, 1, 0))
    shared = {}
    for k in order:
        columns = columns_of(k)
        shared[k] = [
            send(
                mine.at[:, columns], theirs.at[j - 1, :, columns],
                mp_send.at[0], mp_recv.at[k, j - 1], {"mp": hop(core, j, mps)},
            )
            for j in range(1, mps)
        ]
    for j in range(1, ins):
        signal(turn, at(z, a, hop(b, j, ins)))
    inform(zs - 2, zs - 2, up, -1, False)
    inform(1, 1, down, 1, False)
    with scope("own"):
        loads[1].wait()
        for k in order[:OWN]:
            acc[columns_of(k), :] = product(mine[:, columns_of(k)], core)

    with scope("loads2"):
        for load in loads[2:4]:
            load.wait()
    block = (core * cols + lax.broadcasted_iota(jnp.int32, (1, cols), 1)) // width
    trig = jnp.zeros((1, cols), jnp.int32)
    for i in range(BLOCKS):
        trig = trig + jnp.where(block == i, flag[0] * mask[0, i], 0)
    weight = trig.astype(jnp.float32)

    def compute(k):
        columns = columns_of(k)
        grad = acc[columns, :] if k in order[:OWN] else product(mine[:, columns], core)
        for j in range(1, mps):
            with scope(f"exwait{k}"):
                shared[k][j - 1].wait_recv()
            grad = grad + product(theirs[j - 1, :, columns], hop(core, mps - j, mps))
        before = old[columns, :].astype(jnp.float32)
        kept[columns, :] = jnp.where(trig > 0, grad, before).astype(jnp.bfloat16)
        change = weight * (grad - before)
        for s in range(2):
            piece = change[:, s * LANES:(s + 1) * LANES].reshape(ins, ins, rows, LANES)
            part[s, k] = piece

    firsts, seconds, thirds = {}, {}, {}

    def group(k):
        if k == zs:
            return part_b, wire_b, one_b, sum_b, two_b, got_b, pl.ds(0, cut)
        return (part.at[:, k], wire.at[:, k], got_one.at[:, k], sum_one.at[:, k],
                wire_two.at[:, k], got_two.at[:, k], late)

    def send_early(k):
        if not cut or not k:
            return
        for s in range(2):
            early[k - 1, s] = encode(part[s, k, :, :, pl.ds(0, cut)])
        send(early.at[k - 1], got_early.at[k - 1],
             early_send.at[0], early_recv.at[k - 1], at(flip(z, k, zs), a, b))

    def sum_early(_):
        if not cut:
            return
        total = [part[s, 0, :, :, pl.ds(0, cut)] for s in range(2)]
        for k in range(zs - 1, 0, -1):
            with scope(f"we{k}"):
                arrive(early_recv.at[k - 1], got_early.at[k - 1])
            for s in range(2):
                total[s] = total[s] + decode(got_early[k - 1, s])
        for s in range(2):
            part_b[s] = total[s]

    def send_one(k):
        if k == zs and not cut:
            return
        whole, code, got, _, _, _, near = group(k)
        for j in range(1, ins):
            bb, aa = hop(b, j, ins), hop(a, j, ins)
            code[0, :, bb] = encode(whole[0, :, bb, near])
            send(code.at[0, :, bb], got.at[0, j - 1],
                 one_send.at[k], one_recv.at[k], at(z, a, bb))
            code[1, aa] = encode(whole[1, aa, :, near])
            send(code.at[1, aa], got.at[1, j - 1],
                 one_send.at[k], one_recv.at[k], at(z, aa, b))

    def send_two(k):
        if k == zs and not cut:
            return
        whole, _, got, sums, code, got_next, near = group(k)
        with scope(f"w2_{k}"):
            arrive(one_recv.at[k], got)
        for s in range(2):
            total = whole[0, :, b, near] if s == 0 else whole[1, a, :, near]
            for j in range(1, ins):
                total = total + decode(got[s, j - 1])
            sums[s] = total
            for j in range(1, ins):
                bb, aa = hop(b, j, ins), hop(a, j, ins)
                there, peer = (aa, at(z, aa, b)) if s == 0 else (bb, at(z, a, bb))
                code[s, there] = encode(sums[s, there])
                send(code.at[s, there], got_next.at[s, j - 1],
                     two_send.at[k // zs], two_recv.at[k], peer)

    def send_three(k):
        if k == zs and not cut:
            return
        _, _, _, sums, _, got, near = group(k)
        with scope(f"w3_{k}"):
            arrive(two_recv.at[k], got)
        for s in range(2):
            total = sums[s, a if s == 0 else b]
            for j in range(1, ins):
                total = total + decode(got[s, j - 1])
            if k % zs == 0:
                own_sum[s, near] = total
            else:
                wire_three[k - 1, s] = encode(total)
        if k % zs:
            send(wire_three.at[k - 1], got_three.at[k - 1],
                 three_send.at[0], three_recv.at[k - 1], at(flip(z, k, zs), a, b))

    def send_all(k, kinds=(False, True)):
        if k == zs and not cut:
            return
        whole, code, _, _, _, _, near = group(k)
        got = got_all_b if k == zs else got_all.at[:, k]
        for j in range(1, ins * ins):
            if (j // ins > 0 and j % ins > 0) not in kinds:
                continue
            aa, bb = hop(a, j // ins, ins), hop(b, j % ins, ins)
            for s in range(2):
                code[s, aa, bb] = encode(whole[s, aa, bb, near])
            send(code.at[:, aa, bb], got.at[:, j - 1],
                 one_send.at[k], one_recv.at[k], at(z, aa, bb))

    def sum_all(k):
        if k == zs and not cut:
            return
        whole, _, _, _, _, _, near = group(k)
        got = got_all_b if k == zs else got_all.at[:, k]
        with scope(f"wy_{k}"):
            arrive(one_recv.at[k], got)
        for s in range(2):
            total = whole[s, a, b, near]
            for j in range(1, ins * ins):
                total = total + decode(got[s, j - 1])
            if k % zs == 0:
                own_sum[s, near] = total
            else:
                wire_three[k - 1, s] = encode(total)
        if k % zs:
            send(wire_three.at[k - 1], got_three.at[k - 1],
                 three_send.at[0], three_recv.at[k - 1], at(flip(z, k, zs), a, b))

    def send_near(k):
        send_all(k, (False,))

    def send_diagonal(k):
        send_all(k, (True,))

    def reach_plane(_):
        pl.semaphore_wait(turn, ins - 1)

    def relay(_):
        inform(1, zs - 3, up, -1, True)
        inform(2, zs - 2, down, 1, True)

    def reach(_):
        inform(0, min(0, zs - 3), up, 0, True)
        inform(max(2, zs - 1), zs - 1, down, 0, True)

    steps = {"C": compute, "P": send_one, "T": send_two, "H": send_three, "W": relay, "V": reach, "Z": send_early, "B": sum_early, "X": send_all, "Y": sum_all, "x": send_near, "d": send_diagonal, "R": reach_plane}
    for step in STEPS:
        with scope(step):
            steps[step[0]]((order + [zs])[int(step[1])])

    arrive(load_sem.at[4], states)
    halves = [pl.ds(s * LANES, LANES) for s in range(2)]

    def update(near, last):
        for s in range(2):
            here = pl.ds(s * LANES, LANES)
            total = own_sum[s, near]
            if last:
                for k in range(1, zs):
                    total = total + decode(got_three[k - 1, s])
            new_aggregate = states[0, near, here] + total
            out_aggregate[near, here] = new_aggregate
            new_one = beta_one * states[2, near, here] + (1.0 - beta_one) * new_aggregate
            new_two = beta_two * states[3, near, here] + (1.0 - beta_two) * new_aggregate * new_aggregate
            out_one[near, here] = new_one
            out_two[near, here] = new_two
            first_hat = new_one / (1.0 - beta_one**STEP)
            second_hat = new_two / (1.0 - beta_two**STEP)
            step = first_hat / (jnp.sqrt(second_hat) + epsilon)
            held = states[1, near, here]
            new_master = held - learn_rate * (step + decay_rate * held)
            out_master[near, here] = new_master
            full[z, a, b, near, here] = new_master.astype(jnp.bfloat16)

    def update_early():
        if not cut:
            return
        near = pl.ds(0, cut)
        update(near, False)
        ref = full.at[z, a, b, near]
        for j in range(1, ins * ins):
            send(ref, ref, ge_send.at[0], ge_recv.at[0],
                 at(z, hop(a, j // ins, ins), hop(b, j % ins, ins)))

    def update_late():
        for k in order[:-1]:
            with scope(f"wz{k}"):
                arrive(three_recv.at[k - 1], got_three.at[k - 1])
        update(late, True)
        ref = full.at[z, a, b, late]
        for k in ZORDER:
            send(ref, ref, gz_send.at[0], gz_recv.at[k - 1], at(flip(z, k, zs), a, b))

    def forward():
        if not cut:
            return
        with scope("wf"):
            arrive(ge_recv.at[0], full.at[z, 0, 0, pl.ds(0, (ins * ins - 1) * cut)])
        ref = full.at[z, :, :, pl.ds(0, cut)]
        for k in range(1, zs):
            send(ref, ref, gf_send.at[0], gf_recv.at[0], at(flip(z, k, zs), a, b))

    def gather_all(k):
        ref = full.at[flip(z, k, zs), a, b, late]
        for j in range(1, ins * ins):
            send(ref, ref, gd_send.at[j - 1], gd_recv.at[j - 1],
                 at(z, hop(a, j // ins, ins), hop(b, j % ins, ins)))

    def gather_short(k):
        zz = flip(z, k, zs)
        for j in range(1, ins):
            bb, aa = hop(b, j, ins), hop(a, j, ins)
            for s, peer in ((0, at(z, aa, b)), (1, at(z, a, bb))):
                ref = full.at[zz, a, b, late, halves[s]]
                send(ref, ref, gs_send.at[0], gs_recv.at[k], peer)

    def gather_long(k):
        zz = flip(z, k, zs)
        with scope(f"wl{k}"):
            arrive(gs_recv.at[k], full.at[zz, pl.ds(0, ins - 1), 0, late])
        for j in range(1, ins):
            bb, aa = hop(b, j, ins), hop(a, j, ins)
            ref = full.at[zz, :, b, late, halves[0]]
            send(ref, ref, gl_send.at[0], gl_recv.at[0], at(z, a, bb))
            ref = full.at[zz, a, :, late, halves[1]]
            send(ref, ref, gl_send.at[0], gl_recv.at[0], at(z, aa, b))

    def blocks(n, *more):
        return full.at[pl.ds(0, n), *more, late]

    def gather(steps):
        counts = {"S": 0, "L": 0, "D": 0}
        for step in steps:
            with scope(step):
                kind, k = step[0], int(step[1])
                if kind == "A":
                    update_late()
                elif kind == "B":
                    update_early()
                elif kind == "F":
                    forward()
                else:
                    counts[kind] += 1
                    if kind == "L":
                        gather_long(k)
                    else:
                        if k:
                            with scope(f"wg{k}"):
                                arrive(gz_recv.at[k - 1], full.at[flip(z, k, zs), a, b, late])
                        (gather_all if kind == "D" else gather_short)(k)
        with scope("final"):
            if counts["L"]:
                some = blocks(counts["L"], pl.ds(0, ins - 1), pl.ds(0, ins))
                arrive(gl_recv.at[0], some)
                arrive(gs_send.at[0], blocks(counts["L"], pl.ds(0, ins - 1), 0))
                arrive(gl_send.at[0], some)
            if counts["D"]:
                for j in range(1, ins * ins):
                    arrive(gd_recv.at[j - 1], blocks(counts["D"], 0, 0))
                    arrive(gd_send.at[j - 1], blocks(counts["D"], 0, 0))

    if GATHER == GATHER_OTHER:
        gather(GATHER)
    else:
        @pl.when(core == 0)
        def _():
            gather(GATHER)

        @pl.when(core > 0)
        def _():
            gather(GATHER_OTHER)
    if cut:
        with scope("final2"):
            arrive(gf_recv.at[0], full.at[pl.ds(0, zs - 1), :, :, pl.ds(0, cut)])
    with scope("sendwait"):
        arrive(mp_send.at[0], theirs)
        for k in order:
            if f"P{order.index(k)}" in STEPS:
                arrive(one_send.at[k], got_one.at[:, k])
            else:
                arrive(one_send.at[k], got_all.at[:, k])
        halved = sum(f"P{i}" in STEPS for i in range(zs))
        if halved:
            arrive(two_send.at[0], got_two.at[:, pl.ds(zs - halved, halved)])
        arrive(three_send.at[0], got_three)
        arrive(gz_send.at[0], blocks(zs - 1, 0, 0))
        if cut:
            arrive(early_send.at[0], got_early)
            if "P4" in STEPS:
                arrive(one_send.at[zs], one_b)
                arrive(two_send.at[1], got_b)
            else:
                arrive(one_send.at[zs], got_all_b)
            arrive(ge_send.at[0], full.at[z, 0, 0, pl.ds(0, (ins * ins - 1) * cut)])
            arrive(gf_send.at[0], full.at[pl.ds(0, zs - 1), :, :, pl.ds(0, cut)])


def write_out(*refs):
    copies = []
    for src, dst in zip(refs[:6], refs[6:12]):
        parts = max(1, src.shape[0] // 512) * SPLIT
        size = src.shape[0] // parts
        for i in range(parts):
            near = pl.ds(i * size, size)
            copies.append(pltpu.make_async_copy(src.at[near], dst.at[near], refs[12].at[len(copies)]))
    with scope("wo_start"):
        for copy in reversed(copies):
            copy.start()
    with scope("wo_wait"):
        for copy in copies:
            copy.wait()


def on_device(
    workers, mps,
    normed, key_grad, stale, worker_flag, block_mask, aggregate, master, moment_one, moment_two
):
    zs, ins = grid_of(workers)
    tokens, depth = normed.shape
    cols = key_grad.shape[1]
    rows = aggregate.shape[0]
    f32, bf16 = jnp.float32, jnp.bfloat16
    dma = pltpu.SemaphoreType.DMA
    hbm = pl.BlockSpec(memory_space=pltpu.HBM)
    far = functools.partial(pltpu.with_memory_space_constraint, memory_space=pltpu.HBM)
    vmem = pl.BlockSpec(memory_space=pltpu.VMEM)
    state = jax.ShapeDtypeStruct((rows, cols), f32)
    cut = early_rows(rows, ins)
    rest, some = rows - cut, max(cut, 16)
    one = (2, zs, ins, ins, rest, LANES)
    two = (2, zs, ins, rest, LANES)
    direct = any(step[0] == "D" for step in GATHER + GATHER_OTHER)
    results = pl.pallas_call(
        functools.partial(kernel, zs, ins, mps, H // BLOCKS),
        out_shape=(
            state, state, state, state,
            jax.ShapeDtypeStruct((zs, ins, ins, rows, cols), bf16),
            jax.ShapeDtypeStruct((depth, cols), bf16),
        ),
        in_specs=[hbm] * 3 + [pl.BlockSpec(memory_space=pltpu.SMEM)] + [hbm] * 5,
        out_specs=(vmem,) * 6,
        scratch_shapes=[
            pltpu.VMEM((tokens, depth), bf16),
            pltpu.VMEM((mps - 1, tokens, depth), bf16),
            pltpu.VMEM(key_grad.shape, bf16),
            pltpu.VMEM((depth, cols), bf16),
            pltpu.VMEM((4, rows, cols), f32),
            pltpu.VMEM((depth, cols), f32),
            pltpu.VMEM((2, zs, ins, ins, rows, LANES), f32),
            pltpu.VMEM(one, WIRE),
            pltpu.VMEM((2, zs, ins - 1, ins, rest, LANES), WIRE),
            pltpu.VMEM(two, f32),
            pltpu.VMEM(two, WIRE),
            pltpu.VMEM((2, zs, ins - 1, rest, LANES), WIRE),
            pltpu.VMEM((zs - 1, 2, rest, LANES), WIRE),
            pltpu.VMEM((2, rows, LANES), f32),
            pltpu.VMEM((zs - 1, 2, rest, LANES), WIRE),
            pltpu.VMEM((zs - 1, 2, ins, ins, some, LANES), WIRE),
            pltpu.VMEM((zs - 1, 2, ins, ins, some, LANES), WIRE),
            pltpu.VMEM((2, ins, ins, some, LANES), f32),
            pltpu.VMEM((2, ins, ins, some, LANES), WIRE),
            pltpu.VMEM((2, ins - 1, ins, some, LANES), WIRE),
            pltpu.VMEM((2, ins, some, LANES), f32),
            pltpu.VMEM((2, ins, some, LANES), WIRE),
            pltpu.VMEM((2, ins - 1, some, LANES), WIRE),
            pltpu.VMEM((2, zs, ins * ins - 1, rest, LANES), WIRE),
            pltpu.VMEM((2, ins * ins - 1, some, LANES), WIRE),
            pltpu.SMEM(block_mask.shape, jnp.int32),
            pltpu.SemaphoreType.REGULAR, pltpu.SemaphoreType.REGULAR, pltpu.SemaphoreType.REGULAR,
            dma((5,)),
            dma((1,)), dma((zs, mps - 1)),
            dma((zs + 1,)), dma((zs + 1,)),
            dma((2,)), dma((zs + 1,)),
            dma((1,)), dma((zs - 1,)),
            dma((1,)), dma((zs - 1,)),
            dma((1,)), dma((zs,)),
            dma((1,)), dma((1,)),
            dma((ins * ins - 1 if direct else 1,)), dma((ins * ins - 1 if direct else 1,)),
            dma((1,)), dma((zs - 1,)),
            dma((1,)), dma((1,)), dma((1,)), dma((1,)),
        ],
        compiler_params=pltpu.CompilerParams(
            collective_id=0, has_side_effects=True, vmem_limit_bytes=48 * 1024 * 1024
        ),
    )(
        far(normed), far(key_grad), far(stale), worker_flag, far(block_mask),
        far(aggregate), far(master), far(moment_one), far(moment_two),
    )
    results = results[:4] + (results[4].reshape(depth, cols), results[5])
    results = pl.pallas_call(
        write_out,
        out_shape=tuple(pltpu.HBM(x.shape, x.dtype) for x in results),
        in_specs=[vmem] * 6,
        out_specs=(hbm,) * 6,
        scratch_shapes=[dma((4 + 2 * max(1, depth // 512) * SPLIT + 4 * SPLIT,))],
        compiler_params=pltpu.CompilerParams(vmem_limit_bytes=2 * 1024 * 1024),
    )(*results)
    return results[:5] + (results[5][None],)


def solution(mesh):
    placed = (
        P(("dp", "mp"), None),
        P("dp", "mp"),
        P("dp", None, "mp"),
        P("dp"),
        P("dp", None),
        P("dp", "mp"),
        P("dp", "mp"),
        P("dp", "mp"),
        P("dp", "mp"),
    )
    return jax.shard_map(
        functools.partial(on_device, mesh.shape["dp"], mesh.shape["mp"]),
        mesh=mesh,
        in_specs=placed,
        out_specs=(
            P("dp", "mp"),
            P("dp", "mp"),
            P("dp", "mp"),
            P("dp", "mp"),
            P(None, "mp"),
            P("dp", None, "mp"),
        ),
        check_vma=False,
    )
```

time: 41.2 us -> 35.8 us (0.87)
  Pallas kernels: 39.7 us -> 34.3 us
    pallas_call x1, Pallas kernels: 38.2 us -> 32.7 us  [on_device(): pl.pallas_call(functools.partial(kernel, zs, ins, mps, H // BLOCKS), out_...]
where the time goes in v1:
time: 35.8 us; the launch traced here: 35.6 us
  Pallas kernels  34.3 us (96%)
  between operations  1.29 us (4%)
    pallas_call x1, Pallas kernels, on_device(): pl.pallas_call(functools.partial(kernel, zs, ins, mps, H // BLOCKS), out_...  32.7 us
    pallas_call x1, Pallas kernels, on_device(): pl.pallas_call(write_out, out_shape=tuple((pltpu.HBM(x.shape, x.dtype) fo...  1.63 us

profile of v1, /device:TPU:0, one launch (start us, length us, event | category | flops | bytes accessed | tf_op | source)
XLA Modules:
  0.0 35.6 jit_solution(12026593171167329604)
XLA Ops:
  1.3 32.7 %shard_map.136 = (f32[128,256]{1,0:T(8,128)S(1)}, f32[128,256]{1,0:T(8,128)S(1)}, f32[128,256]{1,0:T(8,128)S(1)}, f32[128,256]{1,0:T(8,128)S(1)}, bf16[4,2,2,128...) custom-call(bf16[192,2048]{1,0:T(8,128)(2,1)} %normed.1, bf16[384,256]{1,0:T(8,128)(2,1)} %key_grad.1, ...), custom_call_target="tpu_custom_call" | custom-call | tf_op jit(solution)/shard_map/pallas_call | solution.py:526
  34.0 1.6 %shard_map.137 = (f32[128,256]{1,0:T(8,128)}, f32[128,256]{1,0:T(8,128)}, f32[128,256]{1,0:T(8,128)}, f32[128,256]{1,0:T(8,128)}, bf16[2048,256]{1,0:T(8,128)(2,1)}, /*index=5*/bf16[2048,256]{1,0:T(8,128)(2,1)}) custom-call(f32[128,256]{1,0:T(8,128)S(1)} %get-tuple-element.18.refs_0_, f32[128,256]{1,0:T(8,128)S(1)} %get-tuple-element.19.refs_1_, ...), custom_call_target="tpu_custom_call" | custom-call | tf_op jit(solution)/shard_map/pallas_call | solution.py:583

commit v2 on v1

--- a/solution.py
+++ b/solution.py
@@ -44,9 +44,10 @@
     return jnp.where(code < 0, -size, size)
 
 
-OWN = 4
+OWN = 0
 SPLIT = 1
-EARLY = 8
+EARLY = 2
+LEAD = 2
 ZORDER = (1, 2, 3)
 
 
@@ -56,19 +57,23 @@
 
 STEPS = (
     "W0", "C0", "x0", "C1", "R0", "d0", "X1", "C2", "X2", "C3", "X3", "V0",
-    "Z0", "Z1", "Z2", "Y0", "Y1", "B0", "X4", "Y2", "Y3", "Y4",
+    "Z0", "Z1", "Z2", "Q0", "G0", "Y0", "Y1", "B0", "X4", "Y2", "Y3", "Y4",
+)
+STEPS_OTHER = (
+    "W0", "C0", "C1", "C2", "C3", "R0", "V0", "Z0", "Z1", "Z2", "K0", "X0",
+    "X1", "X2", "X3", "Y0", "Y1", "B0", "X4", "Y2", "Y3", "Y4",
 )
 GATHER = (
-    "B0", "A0", "D0", "F0", "D1", "D3", "D2",
+    "B0", "E0", "A0", "D0", "F0", "D1", "D3", "D2",
 )
 GATHER_OTHER = (
-    "B0", "A0", "D0", "F0", "D1", "D3", "D2",
+    "B0", "E0", "A0", "D0", "F0", "D1", "D3", "D2",
 )
 
 
-def early_rows(rows, ins):
-    size = rows // EARLY if EARLY else 0
-    return 0 if size % 16 or (ins * ins - 1) * size > rows else size
+def early_rows(rows, ins, part):
+    size = rows * part // 16
+    return 0 if size % 8 or (ins * ins - 1) * size > rows else size
 
 
 def flip(base, j, size):
@@ -89,7 +94,7 @@
     mine, theirs, kgrad, old, states, acc,
     part, wire, got_one, sum_one, wire_two, got_two, wire_three, own_sum, got_three,
     early, got_early, part_b, wire_b, one_b, sum_b, two_b, got_b, got_all, got_all_b,
-    mask, up, down, turn, load_sem, mp_send, mp_recv, one_send, one_recv, two_send, two_recv,
+    mask, up, down, turn, gate, load_sem, mp_send, mp_recv, one_send, one_recv, two_send, two_recv,
     three_send, three_recv, gz_send, gz_recv, gs_send, gs_recv, gl_send, gl_recv,
     gd_send, gd_recv, early_send, early_recv, ge_send, ge_recv, gf_send, gf_recv,
 ):
@@ -99,8 +104,8 @@
     tokens = normed.shape[0]
     slab = normed.shape[1] // zs
     rows = slab // (ins * ins)
-    cut = early_rows(rows, ins)
-    late = pl.ds(cut, rows - cut)
+    cut, lead = early_rows(rows, ins, EARLY), early_rows(rows, ins, LEAD)
+    late, behind = pl.ds(cut, rows - cut), pl.ds(lead, rows - lead)
     cols = key_grad.shape[1]
 
     def at(zz, aa, bb):
@@ -165,6 +170,10 @@
 
     with scope("loads"):
         loads[0].wait()
+    with scope("own0"):
+        loads[1].wait()
+        for k in order[:OWN]:
+            acc[columns_of(k), :] = product(mine[:, columns_of(k)], core)
     with scope("barrier"):
         pl.semaphore_wait(barrier, len(peers) + jnp.where(z > 0, 1, 0) + jnp.where(z < zs - 1, 1, 0))
     shared = {}
@@ -182,8 +191,7 @@
     inform(zs - 2, zs - 2, up, -1, False)
     inform(1, 1, down, 1, False)
     with scope("own"):
-        loads[1].wait()
-        for k in order[:OWN]:
+        for k in order[OWN:]:
             acc[columns_of(k), :] = product(mine[:, columns_of(k)], core)
 
     with scope("loads2"):
@@ -197,7 +205,7 @@
 
     def compute(k):
         columns = columns_of(k)
-        grad = acc[columns, :] if k in order[:OWN] else product(mine[:, columns], core)
+        grad = acc[columns, :]
         for j in range(1, mps):
             with scope(f"exwait{k}"):
                 shared[k][j - 1].wait_recv()
@@ -325,6 +333,16 @@
     def send_diagonal(k):
         send_all(k, (True,))
 
+    def sent(k):
+        arrive(one_send.at[k], got_all.at[:, k])
+
+    def give(_):
+        if mps > 1:
+            signal(gate, {"mp": core + 1})
+
+    def take(_):
+        pl.semaphore_wait(gate, 1)
+
     def reach_plane(_):
         pl.semaphore_wait(turn, ins - 1)
 
@@ -336,10 +354,25 @@
         inform(0, min(0, zs - 3), up, 0, True)
         inform(max(2, zs - 1), zs - 1, down, 0, True)
 
-    steps = {"C": compute, "P": send_one, "T": send_two, "H": send_three, "W": relay, "V": reach, "Z": send_early, "B": sum_early, "X": send_all, "Y": sum_all, "x": send_near, "d": send_diagonal, "R": reach_plane}
-    for step in STEPS:
-        with scope(step):
-            steps[step[0]]((order + [zs])[int(step[1])])
+    steps = {"C": compute, "P": send_one, "T": send_two, "H": send_three, "W": relay, "V": reach, "Z": send_early, "B": sum_early, "X": send_all, "Y": sum_all, "x": send_near, "d": send_diagonal, "R": reach_plane, "Q": sent, "G": give, "K": take}
+    def reduce(names):
+        for name in names:
+            with scope(name):
+                steps[name[0]]((order + [zs])[int(name[1])])
+
+    def by_core(run, one, other):
+        if one == other:
+            return run(one)
+
+        @pl.when(core == 0)
+        def _():
+            run(one)
+
+        @pl.when(core > 0)
+        def _():
+            run(other)
+
+    by_core(reduce, STEPS, STEPS_OTHER)
 
     arrive(load_sem.at[4], states)
     halves = [pl.ds(s * LANES, LANES) for s in range(2)]
@@ -368,9 +401,12 @@
     def update_early():
         if not cut:
             return
-        near = pl.ds(0, cut)
-        update(near, False)
-        ref = full.at[z, a, b, near]
+        update(pl.ds(0, cut), False)
+
+    def share():
+        if not lead:
+            return
+        ref = full.at[z, a, b, pl.ds(0, lead)]
         for j in range(1, ins * ins):
             send(ref, ref, ge_send.at[0], ge_recv.at[0],
                  at(z, hop(a, j // ins, ins), hop(b, j % ins, ins)))
@@ -380,21 +416,21 @@
             with scope(f"wz{k}"):
                 arrive(three_recv.at[k - 1], got_three.at[k - 1])
         update(late, True)
-        ref = full.at[z, a, b, late]
+        ref = full.at[z, a, b, behind]
         for k in ZORDER:
             send(ref, ref, gz_send.at[0], gz_recv.at[k - 1], at(flip(z, k, zs), a, b))
 
     def forward():
-        if not cut:
+        if not lead:
             return
         with scope("wf"):
-            arrive(ge_recv.at[0], full.at[z, 0, 0, pl.ds(0, (ins * ins - 1) * cut)])
-        ref = full.at[z, :, :, pl.ds(0, cut)]
+            arrive(ge_recv.at[0], full.at[z, 0, 0, pl.ds(0, (ins * ins - 1) * lead)])
+        ref = full.at[z, :, :, pl.ds(0, lead)]
         for k in range(1, zs):
             send(ref, ref, gf_send.at[0], gf_recv.at[0], at(flip(z, k, zs), a, b))
 
     def gather_all(k):
-        ref = full.at[flip(z, k, zs), a, b, late]
+        ref = full.at[flip(z, k, zs), a, b, behind]
         for j in range(1, ins * ins):
             send(ref, ref, gd_send.at[j - 1], gd_recv.at[j - 1],
                  at(z, hop(a, j // ins, ins), hop(b, j % ins, ins)))
@@ -404,22 +440,22 @@
         for j in range(1, ins):
             bb, aa = hop(b, j, ins), hop(a, j, ins)
             for s, peer in ((0, at(z, aa, b)), (1, at(z, a, bb))):
-                ref = full.at[zz, a, b, late, halves[s]]
+                ref = full.at[zz, a, b, behind, halves[s]]
                 send(ref, ref, gs_send.at[0], gs_recv.at[k], peer)
 
     def gather_long(k):
         zz = flip(z, k, zs)
         with scope(f"wl{k}"):
-            arrive(gs_recv.at[k], full.at[zz, pl.ds(0, ins - 1), 0, late])
+            arrive(gs_recv.at[k], full.at[zz, pl.ds(0, ins - 1), 0, behind])
         for j in range(1, ins):
             bb, aa = hop(b, j, ins), hop(a, j, ins)
-            ref = full.at[zz, :, b, late, halves[0]]
+            ref = full.at[zz, :, b, behind, halves[0]]
             send(ref, ref, gl_send.at[0], gl_recv.at[0], at(z, a, bb))
-            ref = full.at[zz, a, :, late, halves[1]]
+            ref = full.at[zz, a, :, behind, halves[1]]
             send(ref, ref, gl_send.at[0], gl_recv.at[0], at(z, aa, b))
 
     def blocks(n, *more):
-        return full.at[pl.ds(0, n), *more, late]
+        return full.at[pl.ds(0, n), *more, behind]
 
     def gather(steps):
         counts = {"S": 0, "L": 0, "D": 0}
@@ -430,6 +466,8 @@
                     update_late()
                 elif kind == "B":
                     update_early()
+                elif kind == "E":
+                    share()
                 elif kind == "F":
                     forward()
                 else:
@@ -439,7 +477,7 @@
                     else:
                         if k:
                             with scope(f"wg{k}"):
-                                arrive(gz_recv.at[k - 1], full.at[flip(z, k, zs), a, b, late])
+                                arrive(gz_recv.at[k - 1], full.at[flip(z, k, zs), a, b, behind])
                         (gather_all if kind == "D" else gather_short)(k)
         with scope("final"):
             if counts["L"]:
@@ -452,24 +490,19 @@
                     arrive(gd_recv.at[j - 1], blocks(counts["D"], 0, 0))
                     arrive(gd_send.at[j - 1], blocks(counts["D"], 0, 0))
 
-    if GATHER == GATHER_OTHER:
-        gather(GATHER)
-    else:
-        @pl.when(core == 0)
-        def _():
-            gather(GATHER)
-
-        @pl.when(core > 0)
-        def _():
-            gather(GATHER_OTHER)
-    if cut:
+    by_core(gather, GATHER, GATHER_OTHER)
+    if lead:
         with scope("final2"):
-            arrive(gf_recv.at[0], full.at[pl.ds(0, zs - 1), :, :, pl.ds(0, cut)])
+            arrive(gf_recv.at[0], full.at[pl.ds(0, zs - 1), :, :, pl.ds(0, lead)])
     with scope("sendwait"):
         arrive(mp_send.at[0], theirs)
-        for k in order:
-            if f"P{order.index(k)}" in STEPS:
+        for i, k in enumerate(order):
+            if f"P{i}" in STEPS:
                 arrive(one_send.at[k], got_one.at[:, k])
+            elif f"Q{i}" in STEPS:
+                @pl.when(core > 0)
+                def _(k=k):
+                    arrive(one_send.at[k], got_all.at[:, k])
             else:
                 arrive(one_send.at[k], got_all.at[:, k])
         halved = sum(f"P{i}" in STEPS for i in range(zs))
@@ -484,8 +517,9 @@
                 arrive(two_send.at[1], got_b)
             else:
                 arrive(one_send.at[zs], got_all_b)
-            arrive(ge_send.at[0], full.at[z, 0, 0, pl.ds(0, (ins * ins - 1) * cut)])
-            arrive(gf_send.at[0], full.at[pl.ds(0, zs - 1), :, :, pl.ds(0, cut)])
+        if lead:
+            arrive(ge_send.at[0], full.at[z, 0, 0, pl.ds(0, (ins * ins - 1) * lead)])
+            arrive(gf_send.at[0], full.at[pl.ds(0, zs - 1), :, :, pl.ds(0, lead)])
 
 
 def write_out(*refs):
@@ -518,7 +552,7 @@
     far = functools.partial(pltpu.with_memory_space_constraint, memory_space=pltpu.HBM)
     vmem = pl.BlockSpec(memory_space=pltpu.VMEM)
     state = jax.ShapeDtypeStruct((rows, cols), f32)
-    cut = early_rows(rows, ins)
+    cut = early_rows(rows, ins, EARLY)
     rest, some = rows - cut, max(cut, 16)
     one = (2, zs, ins, ins, rest, LANES)
     two = (2, zs, ins, rest, LANES)
@@ -560,6 +594,7 @@
             pltpu.VMEM((2, ins * ins - 1, some, LANES), WIRE),
             pltpu.SMEM(block_mask.shape, jnp.int32),
             pltpu.SemaphoreType.REGULAR, pltpu.SemaphoreType.REGULAR, pltpu.SemaphoreType.REGULAR,
+            pltpu.SemaphoreType.REGULAR,
             dma((5,)),
             dma((1,)), dma((zs, mps - 1)),
             dma((zs + 1,)), dma((zs + 1,)),

time: 35.8 us -> 34.9 us (0.975); the launches traced: 35.6 us -> 34.2 us
  Pallas kernels: 34.3 us -> 32.9 us
    pallas_call x1, Pallas kernels: 32.7 us -> 31.3 us  [on_device(): pl.pallas_call(functools.partial(kernel, zs, ins, mps, H // BLOCKS), out_...]
where the time goes in v2:
time: 34.9 us; the launch traced here: 34.2 us
  Pallas kernels  32.9 us (94%)
  between operations  1.29 us (4%)
    pallas_call x1, Pallas kernels, on_device(): pl.pallas_call(functools.partial(kernel, zs, ins, mps, H // BLOCKS), out_...  31.3 us
    pallas_call x1, Pallas kernels, on_device(): pl.pallas_call(write_out, out_shape=tuple((pltpu.HBM(x.shape, x.dtype) fo...  1.63 us

profile of v2, /device:TPU:0, one launch (start us, length us, event | category | flops | bytes accessed | tf_op | source)
XLA Modules:
  0.0 34.2 jit_solution(4035523062727016573)
XLA Ops:
  1.3 31.3 %shard_map.136 = (f32[128,256]{1,0:T(8,128)S(1)}, f32[128,256]{1,0:T(8,128)S(1)}, f32[128,256]{1,0:T(8,128)S(1)}, f32[128,256]{1,0:T(8,128)S(1)}, bf16[4,2,2,128...) custom-call(bf16[192,2048]{1,0:T(8,128)(2,1)} %normed.1, bf16[384,256]{1,0:T(8,128)(2,1)} %key_grad.1, ...), custom_call_target="tpu_custom_call" | custom-call | tf_op jit(solution)/shard_map/pallas_call | solution.py:560
  32.6 1.6 %shard_map.137 = (f32[128,256]{1,0:T(8,128)}, f32[128,256]{1,0:T(8,128)}, f32[128,256]{1,0:T(8,128)}, f32[128,256]{1,0:T(8,128)}, bf16[2048,256]{1,0:T(8,128)(2,1)}, /*index=5*/bf16[2048,256]{1,0:T(8,128)(2,1)}) custom-call(f32[128,256]{1,0:T(8,128)S(1)} %get-tuple-element.18.refs_0_, f32[128,256]{1,0:T(8,128)S(1)} %get-tuple-element.19.refs_1_, ...), custom_call_target="tpu_custom_call" | custom-call | tf_op jit(solution)/shard_map/pallas_call | solution.py:618

commit v3 on v2

--- a/solution.py
+++ b/solution.py
@@ -45,9 +45,8 @@
 
 
 OWN = 0
-SPLIT = 1
 EARLY = 2
-LEAD = 2
+LEAD = 4
 ZORDER = (1, 2, 3)
 
 
@@ -56,18 +55,18 @@
 
 
 STEPS = (
-    "W0", "C0", "x0", "C1", "R0", "d0", "X1", "C2", "X2", "C3", "X3", "V0",
-    "Z0", "Z1", "Z2", "Q0", "G0", "Y0", "Y1", "B0", "X4", "Y2", "Y3", "Y4",
+    "W0", "C0", "x0", "C1", "R0", "d0", "X1", "C2", "X2", "C3", "X3", "Z2",
+    "V0", "Z0", "Z1", "Q0", "G0", "Y0", "Y1", "B0", "X4", "Y2", "Y3", "Y4",
 )
 STEPS_OTHER = (
-    "W0", "C0", "C1", "C2", "C3", "R0", "V0", "Z0", "Z1", "Z2", "K0", "X0",
-    "X1", "X2", "X3", "Y0", "Y1", "B0", "X4", "Y2", "Y3", "Y4",
+    "W0", "C0", "C1", "C2", "C3", "R0", "V0", "K0", "X0", "X1", "X2", "X3",
+    "Z0", "Z1", "Z2", "Y0", "Y1", "B0", "X4", "Y2", "Y3", "Y4",
 )
 GATHER = (
-    "B0", "E0", "A0", "D0", "F0", "D1", "D3", "D2",
+    "B0", "A0", "E0", "D0", "D1", "F0", "D3", "D2",
 )
 GATHER_OTHER = (
-    "B0", "E0", "A0", "D0", "F0", "D1", "D3", "D2",
+    "B0", "A0", "E0", "D0", "D1", "F0", "D3", "D2",
 )
 
 
@@ -92,11 +91,10 @@
     normed, key_grad, stale, flag, far_mask, aggregate, master, moment_one, moment_two,
     out_aggregate, out_master, out_one, out_two, full, kept,
     mine, theirs, kgrad, old, states, acc,
-    part, wire, got_one, sum_one, wire_two, got_two, wire_three, own_sum, got_three,
-    early, got_early, part_b, wire_b, one_b, sum_b, two_b, got_b, got_all, got_all_b,
-    mask, up, down, turn, gate, load_sem, mp_send, mp_recv, one_send, one_recv, two_send, two_recv,
-    three_send, three_recv, gz_send, gz_recv, gs_send, gs_recv, gl_send, gl_recv,
-    gd_send, gd_recv, early_send, early_recv, ge_send, ge_recv, gf_send, gf_recv,
+    part, wire, got_all, wire_three, own_sum, got_three,
+    early, got_early, part_b, wire_b, got_all_b,
+    mask, up, down, turn, gate, load_sem, mp_send, mp_recv, one_send, one_recv,
+    three_send, three_recv, gz_send, gz_recv, gd_send, gd_recv, early_send, early_recv, ge_send, ge_recv, gf_send, gf_recv,
 ):
     me = lax.axis_index("dp")
     core = lax.axis_index("mp")
@@ -221,9 +219,8 @@
 
     def group(k):
         if k == zs:
-            return part_b, wire_b, one_b, sum_b, two_b, got_b, pl.ds(0, cut)
-        return (part.at[:, k], wire.at[:, k], got_one.at[:, k], sum_one.at[:, k],
-                wire_two.at[:, k], got_two.at[:, k], late)
+            return part_b, wire_b, got_all_b, pl.ds(0, cut)
+        return part.at[:, k], wire.at[:, k], got_all.at[:, k], late
 
     def send_early(k):
         if not cut or not k:
@@ -245,60 +242,10 @@
         for s in range(2):
             part_b[s] = total[s]
 
-    def send_one(k):
-        if k == zs and not cut:
-            return
-        whole, code, got, _, _, _, near = group(k)
-        for j in range(1, ins):
-            bb, aa = hop(b, j, ins), hop(a, j, ins)
-            code[0, :, bb] = encode(whole[0, :, bb, near])
-            send(code.at[0, :, bb], got.at[0, j - 1],
-                 one_send.at[k], one_recv.at[k], at(z, a, bb))
-            code[1, aa] = encode(whole[1, aa, :, near])
-            send(code.at[1, aa], got.at[1, j - 1],
-                 one_send.at[k], one_recv.at[k], at(z, aa, b))
-
-    def send_two(k):
-        if k == zs and not cut:
-            return
-        whole, _, got, sums, code, got_next, near = group(k)
-        with scope(f"w2_{k}"):
-            arrive(one_recv.at[k], got)
-        for s in range(2):
-            total = whole[0, :, b, near] if s == 0 else whole[1, a, :, near]
-            for j in range(1, ins):
-                total = total + decode(got[s, j - 1])
-            sums[s] = total
-            for j in range(1, ins):
-                bb, aa = hop(b, j, ins), hop(a, j, ins)
-                there, peer = (aa, at(z, aa, b)) if s == 0 else (bb, at(z, a, bb))
-                code[s, there] = encode(sums[s, there])
-                send(code.at[s, there], got_next.at[s, j - 1],
-                     two_send.at[k // zs], two_recv.at[k], peer)
-
-    def send_three(k):
-        if k == zs and not cut:
-            return
-        _, _, _, sums, _, got, near = group(k)
-        with scope(f"w3_{k}"):
-            arrive(two_recv.at[k], got)
-        for s in range(2):
-            total = sums[s, a if s == 0 else b]
-            for j in range(1, ins):
-                total = total + decode(got[s, j - 1])
-            if k % zs == 0:
-                own_sum[s, near] = total
-            else:
-                wire_three[k - 1, s] = encode(total)
-        if k % zs:
-            send(wire_three.at[k - 1], got_three.at[k - 1],
-                 three_send.at[0], three_recv.at[k - 1], at(flip(z, k, zs), a, b))
-
     def send_all(k, kinds=(False, True)):
         if k == zs and not cut:
             return
-        whole, code, _, _, _, _, near = group(k)
-        got = got_all_b if k == zs else got_all.at[:, k]
+        whole, code, got, near = group(k)
         for j in range(1, ins * ins):
             if (j // ins > 0 and j % ins > 0) not in kinds:
                 continue
@@ -311,8 +258,7 @@
     def sum_all(k):
         if k == zs and not cut:
             return
-        whole, _, _, _, _, _, near = group(k)
-        got = got_all_b if k == zs else got_all.at[:, k]
+        whole, _, got, near = group(k)
         with scope(f"wy_{k}"):
             arrive(one_recv.at[k], got)
         for s in range(2):
@@ -354,7 +300,7 @@
         inform(0, min(0, zs - 3), up, 0, True)
         inform(max(2, zs - 1), zs - 1, down, 0, True)
 
-    steps = {"C": compute, "P": send_one, "T": send_two, "H": send_three, "W": relay, "V": reach, "Z": send_early, "B": sum_early, "X": send_all, "Y": sum_all, "x": send_near, "d": send_diagonal, "R": reach_plane, "Q": sent, "G": give, "K": take}
+    steps = {"C": compute, "W": relay, "V": reach, "Z": send_early, "B": sum_early, "X": send_all, "Y": sum_all, "x": send_near, "d": send_diagonal, "R": reach_plane, "Q": sent, "G": give, "K": take}
     def reduce(names):
         for name in names:
             with scope(name):
@@ -372,10 +318,16 @@
         def _():
             run(other)
 
+    def drain(names):
+        for i, k in enumerate(order):
+            if f"Q{i}" not in names:
+                sent(k)
+        if cut:
+            arrive(one_send.at[zs], got_all_b)
+
     by_core(reduce, STEPS, STEPS_OTHER)
 
     arrive(load_sem.at[4], states)
-    halves = [pl.ds(s * LANES, LANES) for s in range(2)]
 
     def update(near, last):
         for s in range(2):
@@ -430,106 +382,50 @@
             send(ref, ref, gf_send.at[0], gf_recv.at[0], at(flip(z, k, zs), a, b))
 
     def gather_all(k):
+        if k:
+            with scope(f"wg{k}"):
+                arrive(gz_recv.at[k - 1], full.at[flip(z, k, zs), a, b, behind])
         ref = full.at[flip(z, k, zs), a, b, behind]
         for j in range(1, ins * ins):
             send(ref, ref, gd_send.at[j - 1], gd_recv.at[j - 1],
                  at(z, hop(a, j // ins, ins), hop(b, j % ins, ins)))
 
-    def gather_short(k):
-        zz = flip(z, k, zs)
-        for j in range(1, ins):
-            bb, aa = hop(b, j, ins), hop(a, j, ins)
-            for s, peer in ((0, at(z, aa, b)), (1, at(z, a, bb))):
-                ref = full.at[zz, a, b, behind, halves[s]]
-                send(ref, ref, gs_send.at[0], gs_recv.at[k], peer)
-
-    def gather_long(k):
-        zz = flip(z, k, zs)
-        with scope(f"wl{k}"):
-            arrive(gs_recv.at[k], full.at[zz, pl.ds(0, ins - 1), 0, behind])
-        for j in range(1, ins):
-            bb, aa = hop(b, j, ins), hop(a, j, ins)
-            ref = full.at[zz, :, b, behind, halves[0]]
-            send(ref, ref, gl_send.at[0], gl_recv.at[0], at(z, a, bb))
-            ref = full.at[zz, a, :, behind, halves[1]]
-            send(ref, ref, gl_send.at[0], gl_recv.at[0], at(z, aa, b))
-
-    def blocks(n, *more):
-        return full.at[pl.ds(0, n), *more, behind]
-
-    def gather(steps):
-        counts = {"S": 0, "L": 0, "D": 0}
-        for step in steps:
-            with scope(step):
-                kind, k = step[0], int(step[1])
-                if kind == "A":
-                    update_late()
-                elif kind == "B":
-                    update_early()
-                elif kind == "E":
-                    share()
-                elif kind == "F":
-                    forward()
+    actions = {"A": update_late, "B": update_early, "E": share, "F": forward}
+
+    def gather(names):
+        for name in names:
+            with scope(name):
+                if name[0] == "D":
+                    gather_all(int(name[1]))
                 else:
-                    counts[kind] += 1
-                    if kind == "L":
-                        gather_long(k)
-                    else:
-                        if k:
-                            with scope(f"wg{k}"):
-                                arrive(gz_recv.at[k - 1], full.at[flip(z, k, zs), a, b, behind])
-                        (gather_all if kind == "D" else gather_short)(k)
-        with scope("final"):
-            if counts["L"]:
-                some = blocks(counts["L"], pl.ds(0, ins - 1), pl.ds(0, ins))
-                arrive(gl_recv.at[0], some)
-                arrive(gs_send.at[0], blocks(counts["L"], pl.ds(0, ins - 1), 0))
-                arrive(gl_send.at[0], some)
-            if counts["D"]:
-                for j in range(1, ins * ins):
-                    arrive(gd_recv.at[j - 1], blocks(counts["D"], 0, 0))
-                    arrive(gd_send.at[j - 1], blocks(counts["D"], 0, 0))
+                    actions[name[0]]()
 
     by_core(gather, GATHER, GATHER_OTHER)
+    with scope("final"):
+        for j in range(1, ins * ins):
+            arrive(gd_recv.at[j - 1], full.at[:, 0, 0, behind])
     if lead:
         with scope("final2"):
             arrive(gf_recv.at[0], full.at[pl.ds(0, zs - 1), :, :, pl.ds(0, lead)])
     with scope("sendwait"):
+        for j in range(1, ins * ins):
+            arrive(gd_send.at[j - 1], full.at[:, 0, 0, behind])
         arrive(mp_send.at[0], theirs)
-        for i, k in enumerate(order):
-            if f"P{i}" in STEPS:
-                arrive(one_send.at[k], got_one.at[:, k])
-            elif f"Q{i}" in STEPS:
-                @pl.when(core > 0)
-                def _(k=k):
-                    arrive(one_send.at[k], got_all.at[:, k])
-            else:
-                arrive(one_send.at[k], got_all.at[:, k])
-        halved = sum(f"P{i}" in STEPS for i in range(zs))
-        if halved:
-            arrive(two_send.at[0], got_two.at[:, pl.ds(zs - halved, halved)])
+        by_core(drain, STEPS, STEPS_OTHER)
         arrive(three_send.at[0], got_three)
-        arrive(gz_send.at[0], blocks(zs - 1, 0, 0))
+        arrive(gz_send.at[0], full.at[pl.ds(0, zs - 1), 0, 0, behind])
         if cut:
             arrive(early_send.at[0], got_early)
-            if "P4" in STEPS:
-                arrive(one_send.at[zs], one_b)
-                arrive(two_send.at[1], got_b)
-            else:
-                arrive(one_send.at[zs], got_all_b)
         if lead:
             arrive(ge_send.at[0], full.at[z, 0, 0, pl.ds(0, (ins * ins - 1) * lead)])
             arrive(gf_send.at[0], full.at[pl.ds(0, zs - 1), :, :, pl.ds(0, lead)])
 
 
 def write_out(*refs):
-    copies = []
-    for src, dst in zip(refs[:6], refs[6:12]):
-        parts = max(1, src.shape[0] // 512) * SPLIT
-        size = src.shape[0] // parts
-        for i in range(parts):
-            near = pl.ds(i * size, size)
-            copies.append(pltpu.make_async_copy(src.at[near], dst.at[near], refs[12].at[len(copies)]))
+    copies = [
+        pltpu.make_async_copy(src, dst, refs[12].at[i])
+        for i, (src, dst) in enumerate(zip(refs[:6], refs[6:12]))
+    ]
     with scope("wo_start"):
         for copy in reversed(copies):
             copy.start()
@@ -554,9 +450,6 @@
     state = jax.ShapeDtypeStruct((rows, cols), f32)
     cut = early_rows(rows, ins, EARLY)
     rest, some = rows - cut, max(cut, 16)
-    one = (2, zs, ins, ins, rest, LANES)
-    two = (2, zs, ins, rest, LANES)
-    direct = any(step[0] == "D" for step in GATHER + GATHER_OTHER)
     results = pl.pallas_call(
         functools.partial(kernel, zs, ins, mps, H // BLOCKS),
         out_shape=(
@@ -574,11 +467,8 @@
             pltpu.VMEM((4, rows, cols), f32),
             pltpu.VMEM((depth, cols), f32),
             pltpu.VMEM((2, zs, ins, ins, rows, LANES), f32),
-            pltpu.VMEM(one, WIRE),
-            pltpu.VMEM((2, zs, ins - 1, ins, rest, LANES), WIRE),
-            pltpu.VMEM(two, f32),
-            pltpu.VMEM(two, WIRE),
-            pltpu.VMEM((2, zs, ins - 1, rest, LANES), WIRE),
+            pltpu.VMEM((2, zs, ins, ins, rest, LANES), WIRE),
+            pltpu.VMEM((2, zs, ins * ins - 1, rest, LANES), WIRE),
             pltpu.VMEM((zs - 1, 2, rest, LANES), WIRE),
             pltpu.VMEM((2, rows, LANES), f32),
             pltpu.VMEM((zs - 1, 2, rest, LANES), WIRE),
@@ -586,11 +476,6 @@
             pltpu.VMEM((zs - 1, 2, ins, ins, some, LANES), WIRE),
             pltpu.VMEM((2, ins, ins, some, LANES), f32),
             pltpu.VMEM((2, ins, ins, some, LANES), WIRE),
-            pltpu.VMEM((2, ins - 1, ins, some, LANES), WIRE),
-            pltpu.VMEM((2, ins, some, LANES), f32),
-            pltpu.VMEM((2, ins, some, LANES), WIRE),
-            pltpu.VMEM((2, ins - 1, some, LANES), WIRE),
-            pltpu.VMEM((2, zs, ins * ins - 1, rest, LANES), WIRE),
             pltpu.VMEM((2, ins * ins - 1, some, LANES), WIRE),
             pltpu.SMEM(block_mask.shape, jnp.int32),
             pltpu.SemaphoreType.REGULAR, pltpu.SemaphoreType.REGULAR, pltpu.SemaphoreType.REGULAR,
@@ -598,12 +483,9 @@
             dma((5,)),
             dma((1,)), dma((zs, mps - 1)),
             dma((zs + 1,)), dma((zs + 1,)),
-            dma((2,)), dma((zs + 1,)),
             dma((1,)), dma((zs - 1,)),
             dma((1,)), dma((zs - 1,)),
-            dma((1,)), dma((zs,)),
-            dma((1,)), dma((1,)),
-            dma((ins * ins - 1 if direct else 1,)), dma((ins * ins - 1 if direct else 1,)),
+            dma((ins * ins - 1,)), dma((ins * ins - 1,)),
             dma((1,)), dma((zs - 1,)),
             dma((1,)), dma((1,)), dma((1,)), dma((1,)),
         ],
@@ -620,7 +502,7 @@
         out_shape=tuple(pltpu.HBM(x.shape, x.dtype) for x in results),
         in_specs=[vmem] * 6,
         out_specs=(hbm,) * 6,
-        scratch_shapes=[dma((4 + 2 * max(1, depth // 512) * SPLIT + 4 * SPLIT,))],
+        scratch_shapes=[dma((6,))],
         compiler_params=pltpu.CompilerParams(vmem_limit_bytes=2 * 1024 * 1024),
     )(*results)
     return results[:5] + (results[5][None],)

time: 34.9 us -> 33.9 us (0.971)
  Pallas kernels: 32.9 us -> 32.1 us
    pallas_call x1, Pallas kernels: 31.3 us -> 30.5 us  [on_device(): pl.pallas_call(functools.partial(kernel, zs, ins, mps, H // BLOCKS), out_...]
where the time goes in v3:
time: 33.9 us; the launch traced here: 33.4 us
  Pallas kernels  32.1 us (95%)
  between operations  1.29 us (4%)
    pallas_call x1, Pallas kernels, on_device(): pl.pallas_call(functools.partial(kernel, zs, ins, mps, H // BLOCKS), out_...  30.5 us
    pallas_call x1, Pallas kernels, on_device(): pl.pallas_call(write_out, out_shape=tuple((pltpu.HBM(x.shape, x.dtype) fo...  1.54 us

profile of v3, /device:TPU:0, one launch (start us, length us, event | category | flops | bytes accessed | tf_op | source)
XLA Modules:
  0.0 33.4 jit_solution(8435296693800571930)
XLA Ops:
  1.3 30.5 %shard_map.136 = (f32[128,256]{1,0:T(8,128)S(1)}, f32[128,256]{1,0:T(8,128)S(1)}, f32[128,256]{1,0:T(8,128)S(1)}, f32[128,256]{1,0:T(8,128)S(1)}, bf16[4,2,2,128...) custom-call(bf16[192,2048]{1,0:T(8,128)(2,1)} %normed.1, bf16[384,256]{1,0:T(8,128)(2,1)} %key_grad.1, ...), custom_call_target="tpu_custom_call" | custom-call | tf_op jit(solution)/shard_map/pallas_call | solution.py:453
  31.8 1.5 %shard_map.137 = (f32[128,256]{1,0:T(8,128)}, f32[128,256]{1,0:T(8,128)}, f32[128,256]{1,0:T(8,128)}, f32[128,256]{1,0:T(8,128)}, bf16[2048,256]{1,0:T(8,128)(2,1)}, /*index=5*/bf16[2048,256]{1,0:T(8,128)(2,1)}) custom-call(f32[128,256]{1,0:T(8,128)S(1)} %get-tuple-element.18.refs_0_, f32[128,256]{1,0:T(8,128)S(1)} %get-tuple-element.19.refs_1_, ...), custom_call_target="tpu_custom_call" | custom-call | tf_op jit(solution)/shard_map/pallas_call | solution.py:500

commit v4 on v3

--- a/solution.py
+++ b/solution.py
@@ -47,7 +47,7 @@
 OWN = 0
 EARLY = 2
 LEAD = 4
-ZORDER = (1, 2, 3)
+HALVED = True
 
 
 def scope(name):
@@ -59,8 +59,8 @@
     "V0", "Z0", "Z1", "Q0", "G0", "Y0", "Y1", "B0", "X4", "Y2", "Y3", "Y4",
 )
 STEPS_OTHER = (
-    "W0", "C0", "C1", "C2", "C3", "R0", "V0", "K0", "X0", "X1", "X2", "X3",
-    "Z0", "Z1", "Z2", "Y0", "Y1", "B0", "X4", "Y2", "Y3", "Y4",
+    "W0", "C0", "C1", "C2", "C3", "R0", "V0", "K0", "X0", "Z0", "X1", "Z1",
+    "X2", "Z2", "X3", "Y0", "Y1", "B0", "X4", "Y2", "Y3", "Y4",
 )
 GATHER = (
     "B0", "A0", "E0", "D0", "D1", "F0", "D3", "D2",
@@ -104,6 +104,9 @@
     rows = slab // (ins * ins)
     cut, lead = early_rows(rows, ins, EARLY), early_rows(rows, ins, LEAD)
     late, behind = pl.ds(cut, rows - cut), pl.ds(lead, rows - lead)
+    half = (rows - lead) // 2
+    edges = [lead, lead + half, rows] if HALVED and half % 8 == 0 else [lead, rows]
+    parts = [pl.ds(low, high - low) for low, high in zip(edges, edges[1:])]
     cols = key_grad.shape[1]
 
     def at(zz, aa, bb):
@@ -329,13 +332,14 @@
 
     arrive(load_sem.at[4], states)
 
-    def update(near, last):
+    def update(low, high, last):
+        near, there = pl.ds(low, high - low), pl.ds(low - cut, high - low)
         for s in range(2):
             here = pl.ds(s * LANES, LANES)
             total = own_sum[s, near]
             if last:
                 for k in range(1, zs):
-                    total = total + decode(got_three[k - 1, s])
+                    total = total + decode(got_three[k - 1, s, there])
             new_aggregate = states[0, near, here] + total
             out_aggregate[near, here] = new_aggregate
             new_one = beta_one * states[2, near, here] + (1.0 - beta_one) * new_aggregate
@@ -353,7 +357,7 @@
     def update_early():
         if not cut:
             return
-        update(pl.ds(0, cut), False)
+        update(0, cut, False)
 
     def share():
         if not lead:
@@ -363,14 +367,17 @@
             send(ref, ref, ge_send.at[0], ge_recv.at[0],
                  at(z, hop(a, j // ins, ins), hop(b, j % ins, ins)))
 
-    def update_late():
+    def update_late(turns):
         for k in order[:-1]:
             with scope(f"wz{k}"):
                 arrive(three_recv.at[k - 1], got_three.at[k - 1])
-        update(late, True)
-        ref = full.at[z, a, b, behind]
-        for k in ZORDER:
-            send(ref, ref, gz_send.at[0], gz_recv.at[k - 1], at(flip(z, k, zs), a, b))
+        low = cut
+        for h, high in enumerate(edges[1:]):
+            update(low, high, True)
+            low = high
+            ref = full.at[z, a, b, parts[h]]
+            for k in turns:
+                send(ref, ref, gz_send.at[0], gz_recv.at[k - 1, h], at(flip(z, k, zs), a, b))
 
     def forward():
         if not lead:
@@ -382,21 +389,24 @@
             send(ref, ref, gf_send.at[0], gf_recv.at[0], at(flip(z, k, zs), a, b))
 
     def gather_all(k):
-        if k:
-            with scope(f"wg{k}"):
-                arrive(gz_recv.at[k - 1], full.at[flip(z, k, zs), a, b, behind])
-        ref = full.at[flip(z, k, zs), a, b, behind]
-        for j in range(1, ins * ins):
-            send(ref, ref, gd_send.at[j - 1], gd_recv.at[j - 1],
-                 at(z, hop(a, j // ins, ins), hop(b, j % ins, ins)))
-
-    actions = {"A": update_late, "B": update_early, "E": share, "F": forward}
+        for h, part_rows in enumerate(parts):
+            ref = full.at[flip(z, k, zs), a, b, part_rows]
+            if k:
+                with scope(f"wg{k}{h}"):
+                    arrive(gz_recv.at[k - 1, h], ref)
+            for j in range(1, ins * ins):
+                send(ref, ref, gd_send.at[j - 1], gd_recv.at[j - 1],
+                     at(z, hop(a, j // ins, ins), hop(b, j % ins, ins)))
+
+    actions = {"B": update_early, "E": share, "F": forward}
 
     def gather(names):
         for name in names:
             with scope(name):
                 if name[0] == "D":
                     gather_all(int(name[1]))
+                elif name[0] == "A":
+                    update_late([k for k in range(1, zs)][:: -1 if name == "A1" else 1])
                 else:
                     actions[name[0]]()
 
@@ -484,7 +494,7 @@
             dma((1,)), dma((zs, mps - 1)),
             dma((zs + 1,)), dma((zs + 1,)),
             dma((1,)), dma((zs - 1,)),
-            dma((1,)), dma((zs - 1,)),
+            dma((1,)), dma((zs - 1, 2)),
             dma((ins * ins - 1,)), dma((ins * ins - 1,)),
             dma((1,)), dma((zs - 1,)),
             dma((1,)), dma((1,)), dma((1,)), dma((1,)),

time: 33.9 us -> 33.4 us (0.985)
  the two profiles are of different devices: /device:TPU:0 before, /device:TPU:1 now
where the time goes in v4:
time: 33.4 us; the launch traced here: 33.2 us
  Pallas kernels  32 us (96%)
  between operations  1.29 us (4%)
    pallas_call x1, Pallas kernels, on_device(): pl.pallas_call(functools.partial(kernel, zs, ins, mps, H // BLOCKS), out_...  30.4 us
    pallas_call x1, Pallas kernels, on_device(): pl.pallas_call(write_out, out_shape=tuple((pltpu.HBM(x.shape, x.dtype) fo...  1.54 us

profile of v4, /device:TPU:1, one launch (start us, length us, event | category | flops | bytes accessed | tf_op | source)
XLA Modules:
  0.0 33.2 jit_solution(16124264035669793188)
XLA Ops:
  1.3 30.4 %shard_map.136 = (f32[128,256]{1,0:T(8,128)S(1)}, f32[128,256]{1,0:T(8,128)S(1)}, f32[128,256]{1,0:T(8,128)S(1)}, f32[128,256]{1,0:T(8,128)S(1)}, bf16[4,2,2,128...) custom-call(bf16[192,2048]{1,0:T(8,128)(2,1)} %normed.1, bf16[384,256]{1,0:T(8,128)(2,1)} %key_grad.1, ...), custom_call_target="tpu_custom_call" | custom-call | tf_op jit(solution)/shard_map/pallas_call | solution.py:463
  31.7 1.5 %shard_map.137 = (f32[128,256]{1,0:T(8,128)}, f32[128,256]{1,0:T(8,128)}, f32[128,256]{1,0:T(8,128)}, f32[128,256]{1,0:T(8,128)}, bf16[2048,256]{1,0:T(8,128)(2,1)}, /*index=5*/bf16[2048,256]{1,0:T(8,128)(2,1)}) custom-call(f32[128,256]{1,0:T(8,128)S(1)} %get-tuple-element.18.refs_0_, f32[128,256]{1,0:T(8,128)S(1)} %get-tuple-element.19.refs_1_, ...), custom_call_target="tpu_custom_call" | custom-call | tf_op jit(solution)/shard_map/pallas_call | solution.py:510
